TPU v7x, 32 devices: a whole 2x2x4 slice. The times are simulated.
32 devices in a mesh: dp: 4 (over y, x), cls: 8 (over z, core).
Axes of the slice: x: 2, y: 2, z: 4, core: 2. Of those that a mesh axis runs over, the one named last changes fastest.
Arguments:
- embeddings: float32 [2048, 512], P('dp'), may hold values from -60 to 60, as said below
- classifier: float32 [131072, 512], P(('dp', 'cls')), may hold values from -60 to 60, as said below
- labels: int32 [2048], replicated, may hold values from 0 to 131071
- row_scale: float32 [2048], replicated, may hold values from 16 to 512
Outputs:
- loss: float32 [2048], P(('dp', 'cls'))
Inputs may be any that keep to these rules, and one draw needn't show every extreme that they name: `embeddings`: rows of different scales. `classifier`: rows of different scales.
All inputs are finite; a program needn't handle non-finite values.
Results may differ from a plain program's by a relative error of at most 0.0003.
Values sent between devices are 32-bit elements; how exact they have to be, the bound alone decides.
A program may use at most 128 MiB of HBM per device.

v0:
```python
import math

import jax
import jax.numpy as jnp
from jax import lax
from jax.sharding import PartitionSpec as P

MARGIN = 0.5
COS_MARGIN = math.cos(MARGIN)
SIN_MARGIN = math.sin(MARGIN)


def unit_rows(values):
    return values * lax.rsqrt(jnp.sum(values * values, axis=-1, keepdims=True) + 1e-06)


def margin_logit(units, picked, scales):
    cosine = jnp.sum(units * picked, axis=-1)
    across = units - cosine[:, None] * picked
    sine = jnp.sqrt(jnp.sum(across * across, axis=-1))
    return scales * (cosine * COS_MARGIN - sine * SIN_MARGIN)


def block_stats(units, rows, class_ids, labels, scales, picked, owned):
    cosine = lax.dot_general(
        units,
        rows,
        (((1,), (1,)), ((), ())),
        precision=lax.Precision.HIGHEST,
        preferred_element_type=jnp.float32,
    )
    target = margin_logit(units, picked, scales)
    hit = labels[:, None] == class_ids[None, :]
    logits = jnp.where(hit, target[:, None], scales[:, None] * cosine)
    peak = jnp.max(logits, axis=1)
    total = jnp.sum(jnp.exp(logits - peak[:, None]), axis=1)
    return (peak, total, jnp.where(owned, target, jnp.zeros_like(target)))


def body(embeddings, classifier, labels, row_scale):
    rows_here = classifier.shape[0]
    units_mine = unit_rows(embeddings)
    normed = unit_rows(classifier)
    offset = lax.axis_index(("dp", "cls")) * rows_here
    class_ids = offset + jnp.arange(rows_here, dtype=jnp.int32)
    owned_all = (labels >= offset) & (labels < offset + rows_here)
    local_all = jnp.clip(labels - offset, 0, rows_here - 1)
    count = labels.shape[0]
    picked = jnp.take(normed, local_all, axis=0)
    stats = block_stats(
        lax.all_gather(units_mine, "dp", axis=0, tiled=True),
        normed,
        class_ids,
        labels,
        row_scale,
        picked,
        owned_all,
    )
    peak, total, target = tuple((fresh for fresh in stats))
    share = count // lax.axis_size(("dp", "cls"))
    first = lax.axis_index(("dp", "cls")) * share
    best = lax.pmax(peak, ("dp", "cls"))
    scaled = total * jnp.exp(peak - best)
    total_mine, target_mine = (
        lax.psum_scatter(scaled, ("dp", "cls"), scatter_dimension=0, tiled=True),
        lax.psum_scatter(target, ("dp", "cls"), scatter_dimension=0, tiled=True),
    )
    return lax.dynamic_slice_in_dim(best, first, share) + jnp.log(total_mine) - target_mine


def solution(mesh):
    placed = (P("dp", None), P(("dp", "cls"), None), P(), P())
    return jax.shard_map(
        body, mesh=mesh, in_specs=placed, out_specs=P(("dp", "cls")), check_vma=False
    )
```

profile of v0, /device:TPU:0, one launch (start us, length us, event | category | flops | bytes accessed | tf_op | source)
XLA Modules:
  0.0 238.2 jit_solution(17074595091030341979)
XLA Ops:
  6.5 0.0 all-gather.2.cloned.1.call-start
  6.5 1.4 multiply_reduce_fusion.3
  7.9 2.4 broadcast_multiply_fusion.1
  10.3 0.0 all-gather.2.cloned.1.call-update
  10.3 0.0 copy-start.1
  10.3 0.9 fusion.1
  11.2 4.1 %multiply_reduce_fusion = f32[4096]{0:T(1024)S(1)} fusion(f32[4096,512]{1,0:T(8,128)} %param.5), kind=kLoop, calls=%fused_computation.4 | loop fusion | flops 4190208 | bytes 8404992 | tf_op jit(solution)/shard_map/reduce_sum | solution.py:14
  15.3 0.8 copy-done.1
  16.1 3.7 %broadcast_multiply_fusion = f32[4096,512]{1,0:T(8,128)} fusion(f32[4096,512]{1,0:T(8,128)S(1)} %copy-done.1, f32[4096]{0:T(1024)S(1)} %add_rsqrt_fusion), kind=kLoop, calls=%fused_computation.7 | loop fusion | flops 2097152 | bytes 16793600 | tf_op jit(solution)/shard_map/mul | solution.py:14
  19.8 0.0 copy-start.3
  19.8 13.7 %gather_fusion = f32[2048,512]{1,0:T(8,128)} fusion(f32[4096,512]{1,0:T(8,128)} %broadcast_multiply_fusion, s32[2048]{0:T(1024)S(1)} %fusion.1), kind=kCustom, calls=%fused_computation | custom fusion | bytes 8396800 | tf_op jit(solution)/shard_map/jit(_take)/gather | solution.py:49
  33.5 0.0 copy-done.3
  33.5 0.0 copy-start.4
  33.5 32.3 %all-gather.2.cloned.1.call-done = f32[2048,512]{1,0:T(8,128)} async-done(((f32[512,512]{1,0:T(8,128)}), f32[2048,512]{1,0:T(8,128)}) %all-gather.2.cloned.1.call-update) | async-done | bytes 4194320 | tf_op jit(solution)/shard_map/all_gather | solution.py:51
  65.8 0.0 copy-start
  65.8 0.0 slice-start
  65.8 0.0 copy-start.2
  65.8 4.1 %multiply_reduce_fusion.2 = f32[2048]{0:T(1024)S(1)} fusion(f32[2048,512]{1,0:T(8,128)} %all-gather.2.cloned.1.call-done, f32[2048,512]{1,0:T(8,128)} %gather_fusion, pred[2048]{0:T(1024)(128)(4,1)S(1)} %compare_and_fusion), kind=kLoop, calls=%fused_computation.6 | loop fusion | flops 3143680 | bytes 8398848 | tf_op jit(solution)/shard_map/reduce_sum | solution.py:18
  69.8 0.6 copy-done
  70.4 0.0 slice-start.1
  70.4 3.6 %multiply_reduce_fusion.1 = f32[2048]{0:T(1024)S(1)} fusion(f32[2048,512]{1,0:T(8,128)} %all-gather.2.cloned.1.call-done, f32[2048,512]{1,0:T(8,128)S(1)} %copy-done, f32[2048]{0:T(1024)S(1)} %multiply_reduce_fusion.2, pred[2048]{0:T(1024)(128)(4,1)S(1)} %compare_and_fusion), kind=kLoop, calls=%fused_computation.5 | loop fusion | flops 5240832 | bytes 8407040 | tf_op jit(solution)/shard_map/reduce_sum | solution.py:20
  74.1 0.0 copy-done.4
  74.1 0.0 slice-done
  74.1 0.1 copy-done.2
  74.2 1.4 slice-done.1
  75.6 59.6 %fusion = (f32[2048]{0:T(1024)S(1)}, f32[2048,4096]{1,0:T(8,128)}) fusion(f32[2048]{0:T(1024)S(1)} %copy-done.4, f32[2048]{0:T(1024)S(1)} %get-tuple-element.8, s32[4096]{0:T(1024)S(1)} %iota_add_fusion, s32[2048]{0:T(1024)S(1)} %copy-done.3, f32[2048,512]{1,0:T(8,128)S(1)} %copy-done.2, f32[4096,512]{1,0:T(8,128)S(1)} %bitcast.3), kind=kOutput, calls=%fused_computation.3 | convolution fusion | flops 51573161984 | bytes 46186496 | tf_op jit(solution)/shard_map/dot_general | solution.py:25
  135.2 39.3 %pmax.7 = f32[2048]{0:T(1024)S(1)} all-reduce(f32[2048]{0:T(1024)S(1)} %get-tuple-element.9), channel_id=1, replica_groups=mesh['dp'=4,'cls'=8] {'dp','cls'}, use_global_device_ids=true, to_apply=%region_5.6 | all-reduce | flops 2048 | bytes 16384 | tf_op jit(solution)/shard_map/pmax | solution.py:62
  174.5 15.0 %exponential_reduce_fusion = f32[2048]{0:T(1024)S(1)} fusion(f32[2048,4096]{1,0:T(8,128)} %get-tuple-element.10, f32[2048]{0:T(1024)S(1)} %get-tuple-element.9, f32[2048]{0:T(1024)S(1)} %copy-done.4, f32[2048]{0:T(1024)S(1)} %get-tuple-element.8, s32[4096]{0:T(1024)S(1)} %iota_add_fusion, s32[2048]{0:T(1024)S(1)} %copy-done.3), kind=kLoop, calls=%fused_computation.1 | loop fusion | flops 41940992 | bytes 33611776 | tf_op jit(solution)/shard_map/reduce_sum | solution.py:36
  189.6 41.1 %all-reduce.2 = (f32[2048]{0:T(1024)S(1)}, f32[2048]{0:T(1024)S(1)}) all-reduce(f32[2048]{0:T(1024)S(1)} %get-tuple-element.7, f32[2048]{0:T(1024)S(1)} %exponential_multiply_fusion), channel_id=3, replica_groups=mesh['dp'=4,'cls'=8] {'dp','cls'}, use_global_device_ids=true, to_apply=%region_8.9.clone | all-reduce | flops 4096 | bytes 32768
  230.7 0.6 dynamic-slice_subtract_fusion
  (7 shorter events, 0.1 us)
Async XLA Ops:
  6.5 59.2 %all-gather.2.cloned.1.call-start = ((), (), s32[]{:S(2)}) async-start(), calls=%async_computation | async-start | bytes 5242880 | tf_op jit(solution)/shard_map/all_gather | solution.py:51
  10.3 5.8 %copy-start.1 = (f32[4096,512]{1,0:T(8,128)S(1)}, f32[4096,512]{1,0:T(8,128)}, u32[]{:S(2)}) copy-start(f32[4096,512]{1,0:T(8,128)} %param.5) | copy-start | bytes 25165828
  19.8 13.7 %copy-start.3 = (s32[2048]{0:T(1024)S(1)}, s32[2048]{0:T(1024)}, u32[]{:S(2)}) copy-start(s32[2048]{0:T(1024)} %param.6) | copy-start | bytes 24580
  33.5 40.6 %copy-start.4 = (f32[2048]{0:T(1024)S(1)}, f32[2048]{0:T(1024)}, u32[]{:S(2)}) copy-start(f32[2048]{0:T(1024)} %param.7) | copy-start | bytes 24580
  65.8 4.7 %copy-start = (f32[2048,512]{1,0:T(8,128)S(1)}, f32[2048,512]{1,0:T(8,128)}, u32[]{:S(2)}) copy-start(f32[2048,512]{1,0:T(8,128)} %gather_fusion) | copy-start | bytes 12582916
  65.8 8.3 %slice-start = ((s8[8388608]{0:T(1024)(128)(4,1)}), s8[4194304]{0:T(1024)(128)(4,1)S(1)}, s32[]{:S(2)}) async-start(s8[8388608]{0:T(1024)(128)(4,1)} %bitcast.2), calls=%async_computation.1 | async-start | bytes 8388608
  65.8 8.4 %copy-start.2 = (f32[2048,512]{1,0:T(8,128)S(1)}, f32[2048,512]{1,0:T(8,128)}, u32[]{:S(2)}) copy-start(f32[2048,512]{1,0:T(8,128)} %all-gather.2.cloned.1.call-done) | copy-start | bytes 12582916
  70.4 5.2 %slice-start.1 = ((s8[8388608]{0:T(1024)(128)(4,1)}), s8[4194304]{0:T(1024)(128)(4,1)S(1)}, s32[]{:S(2)}) async-start(s8[8388608]{0:T(1024)(128)(4,1)} %bitcast.2), calls=%async_computation.2 | async-start | bytes 8388608
Sparse Core Ops, SparseCore 0:
  10.4 55.2 all-gather.1
where the time goes:
time: 239 us; the launch traced here: 238 us
  blocking collectives  80.4 us (34%)
  matrix products  59.6 us (25%)
  other arithmetic  35.8 us (15%)
  waiting for transfers between devices  32.3 us (14%)
  local copies, waits for them, and re-layouts  16.6 us (7%)
  between operations  13.5 us (6%)
    dot_general x1, matrix products, block_stats(): lax.dot_general(units, rows, (((1,), (1,)), ((), ())), precision=lax.Prec...  59.6 us
    unnamed x1, blocking collectives  41.1 us
    pmax x1, blocking collectives, body(): best = lax.pmax(peak, ('dp', 'cls'))  39.3 us
    all_gather x1, waiting for transfers between devices, body(): lax.all_gather(units_mine, 'dp', axis=0, tiled=True)  32.3 us
    reduce_sum x1, other arithmetic, block_stats(): total = jnp.sum(jnp.exp(logits - peak[:, None]), axis=1)  15 us
    gather x1, local copies, waits for them, and re-layouts, body(): picked = jnp.take(normed, local_all, axis=0)  13.7 us
    mul x2, other arithmetic, unit_rows(): values * lax.rsqrt(jnp.sum(values * values, axis=-1, keepdims=True) + 1e-06)  6.05 us
    reduce_sum x2, other arithmetic, unit_rows(): jnp.sum(values * values, axis=-1, keepdims=True) + 1e-06  5.52 us
  transfers between devices with their start and end apart: 1, of which 1 were waited for; matrix products, arithmetic and copies ran while one was open for 9% of the time, Pallas kernels for 0%

commit v1 on v0

v1 whole, which is shorter than its diff:
```python
import functools
import math

import jax
import jax.numpy as jnp
from jax import lax
from jax.experimental import pallas as pl
from jax.experimental.pallas import tpu as pltpu
from jax.sharding import PartitionSpec as P

MARGIN = 0.5
COS_MARGIN = math.cos(MARGIN)
SIN_MARGIN = math.sin(MARGIN)
LOG2E = math.log2(math.e)
LN2 = math.log(2.0)
LOW = -1e30
MESH = pl.DeviceIdType.MESH


def kernel(ndp, ncls, chunk, emb_hbm, cls_hbm, lab_sm, lab_ref, scale_ref, out_ref,
           emb, raw, unit_w, picks, unit_e, buf0, buf1, stats, got,
           emb_sem, raw_sem, xs, xr, ys, yr, ds, dr, ss, sr):
    dp, cls = lax.axis_index("dp"), lax.axis_index("cls")
    core = lax.rem(cls, 2)
    ndev = ndp * ncls
    me = dp * ncls + cls
    rows, width = cls_hbm.shape
    half = width // 2
    piece = emb_hbm.shape[0] // 4
    groups, lanes = lab_ref.shape
    nchunk = rows // chunk
    offset = me * rows

    barrier = pltpu.get_barrier_semaphore()

    @pl.loop(1, ndev)
    def _(k):
        to = lax.rem(me + k, ndev)
        pl.semaphore_signal(barrier, inc=1, device_id=(to // ncls, lax.rem(to, ncls)), device_id_type=MESH)

    emb_in = [
        pltpu.make_async_copy(emb_hbm.at[:, pl.ds(c * half, half)], emb.at[0, c], emb_sem.at[c])
        for c in range(2)
    ]
    for copy in emb_in:
        copy.start()
    raw_in = [
        pltpu.make_async_copy(raw_hbm, raw.at[pl.ds(i * chunk, chunk)], raw_sem.at[i])
        for i in range(nchunk)
        for raw_hbm in [cls_hbm.at[pl.ds(i * chunk, chunk)]]
    ]
    for copy in raw_in:
        copy.start()

    def prepare(i):
        raw_in[i].wait()

        @pl.loop(0, chunk // 64)
        def _(b):
            at = pl.ds(pl.multiple_of(i * chunk + b * 64, 64), 64)
            w = raw[at, :]
            inv = lax.rsqrt(jnp.sum(w * w, axis=1, keepdims=True) + 1e-06)
            unit_w[at, :] = (w * inv).astype(jnp.bfloat16)

    early = nchunk // 2
    for i in range(early):
        prepare(i)
    for copy in emb_in:
        copy.wait()
    pl.semaphore_wait(barrier, ndev - 1)

    to_x = (dp ^ 1, cls)
    to_y = (dp ^ 2, cls)
    partner = (dp, cls ^ 1)

    def part(slot, j):
        return emb.at[slot, core, pl.ds(j * piece, piece)]

    def send(src, dst, s, r, k, to):
        copy = pltpu.make_async_remote_copy(
            src_ref=part(*src), dst_ref=part(*dst), send_sem=s.at[k], recv_sem=r.at[k],
            device_id=to, device_id_type=MESH,
        )
        copy.start()
        return copy

    x_slot = [(1, 0), (1, 1), (1, 2), (1, 3), (3, 2), (3, 3)]
    y_slot = [(2, 2), (2, 3), (2, 0), (2, 1), (3, 0), (3, 1)]
    x_copy, y_copy, d_copy = [], [], []
    for k in range(4):
        x_copy.append(send((0, x_slot[k][1]), x_slot[k], xs, xr, k, to_x))
        y_copy.append(send((0, y_slot[k][1]), y_slot[k], ys, yr, k, to_y))
    for i in range(early, nchunk):
        prepare(i)

    def forward(k):
        x_copy[k].wait_recv()
        y_copy[k].wait_recv()
        if k < 2:
            x_copy.append(send(y_slot[k], x_slot[k + 4], xs, xr, k + 4, to_x))
            y_copy.append(send(x_slot[k], y_slot[k + 4], ys, yr, k + 4, to_y))
        d_copy.append(send(x_slot[k], x_slot[k], ds, dr, 2 * k, partner))
        d_copy.append(send(y_slot[k], y_slot[k], ds, dr, 2 * k + 1, partner))

    def unit_rows(pair):
        left = jnp.concatenate([emb[s, 0, pl.ds(j * piece, piece), :] for s, j in pair], axis=0)
        right = jnp.concatenate([emb[s, 1, pl.ds(j * piece, piece), :] for s, j in pair], axis=0)
        values = jnp.concatenate([left, right], axis=1)
        return values * lax.rsqrt(jnp.sum(values * values, axis=1, keepdims=True) + 1e-06)

    def compute(pair):
        group = [(dp ^ s) * 4 + j for s, j in pair]
        unit_e[...] = unit_rows(pair).astype(jnp.bfloat16)
        local = jnp.concatenate([lab_ref[pl.ds(g, 1), :] for g in group], axis=1) - offset
        scale = jnp.concatenate([scale_ref[pl.ds(g, 1), :] for g in group], axis=1)
        scale2 = scale * LOG2E
        wide = 2 * piece
        share = wide // nchunk

        def dot(i, buf):
            at = pl.ds(pl.multiple_of(i * chunk, chunk), chunk)
            buf[...] = lax.dot_general(
                unit_w[at, :], unit_e[...], (((1,), (1,)), ((), ())),
                preferred_element_type=jnp.float32,
            )
            first = i * share
            base = jnp.where(first < piece, group[0] * piece, group[1] * piece - piece) + first
            for t in range(share):
                here = jnp.clip(lab_sm[base + t] - offset, 0, rows - 1)
                picks[pl.ds(first + t, 1), :] = raw[pl.ds(here, 1), :]

        def fold(i, buf, peak, total):
            ids = lax.broadcasted_iota(jnp.int32, (chunk, wide), 0)
            z = jnp.where(ids == local - i * chunk, LOW, buf[...] * scale2)
            z = z.reshape(chunk // 8, 8, wide)
            fresh = jnp.maximum(peak, jnp.max(z, axis=0))
            total = total * jnp.exp2(peak - fresh) + jnp.sum(jnp.exp2(z - fresh[None]), axis=0)
            return fresh, total

        dot(0, buf0)

        def both(h, carry):
            i = 2 * h
            dot(i + 1, buf1)
            carry = fold(i, buf0, *carry)
            dot(i + 2, buf0)
            return fold(i + 1, buf1, *carry)

        start = (jnp.full((8, wide), LOW, jnp.float32), jnp.zeros((8, wide), jnp.float32))
        carry = lax.fori_loop(0, nchunk // 2 - 1, both, start)
        dot(nchunk - 1, buf1)
        carry = fold(nchunk - 2, buf0, *carry)
        peak, total = fold(nchunk - 1, buf1, *carry)
        best = jnp.max(peak, axis=0, keepdims=True)
        total = jnp.sum(total * jnp.exp2(peak - best), axis=0, keepdims=True)

        units = unit_rows(pair)
        picked = picks[...]
        picked = picked * lax.rsqrt(jnp.sum(picked * picked, axis=1, keepdims=True) + 1e-06)
        cosine = jnp.sum(units * picked, axis=1, keepdims=True)
        across = units - cosine * picked
        sine = jnp.sqrt(jnp.sum(across * across, axis=1, keepdims=True))
        target = cosine * COS_MARGIN - sine * SIN_MARGIN
        target = jnp.transpose(jnp.broadcast_to(target, (wide, 128)))[0:1, :]
        owned = (local >= 0) & (local < rows)
        target = jnp.where(owned, scale * target, 0.0)
        for n, g in enumerate(group):
            cut = slice(n * piece, (n + 1) * piece)
            stats[pl.ds(g, 1), 0:1, :] = best[:, cut][None]
            stats[pl.ds(g, 1), 1:2, :] = total[:, cut][None]
            stats[pl.ds(g, 1), 2:3, :] = target[:, cut][None]

    def compute_stage(k):
        d_copy[2 * k].wait_recv()
        d_copy[2 * k + 1].wait_recv()
        compute([x_slot[k], y_slot[k]])

    compute([(0, 0), (0, 1)])
    forward(0)
    compute([(0, 2), (0, 3)])
    for k in range(5):
        forward(k + 1)
        compute_stage(k)
    compute_stage(5)

    share = groups * lanes // ndev
    per = lanes // share

    def outgoing(k):
        to = lax.rem(me + k, ndev)
        return pltpu.make_async_remote_copy(
            src_ref=stats.at[to // per], dst_ref=got.at[k], send_sem=ss, recv_sem=sr,
            device_id=(to // ncls, lax.rem(to, ncls)), device_id_type=MESH,
        )

    @pl.loop(1, ndev)
    def _(k):
        outgoing(k).start()

    got[0] = stats[me // per]
    for copy in x_copy + y_copy + d_copy:
        copy.wait_send()
    rest = got.at[pl.ds(1, ndev - 1)]
    pltpu.make_async_copy(rest, rest, ss).wait()
    pltpu.make_async_copy(rest, rest, sr).wait()

    everyone = got[...]
    peaks, totals = everyone[:, 0, :], everyone[:, 1, :]
    target = jnp.sum(everyone[:, 2, :], axis=0, keepdims=True)
    best = jnp.maximum(jnp.max(peaks, axis=0, keepdims=True), target * LOG2E)
    total = jnp.sum(totals * jnp.exp2(peaks - best), axis=0, keepdims=True) + jnp.exp2(target * LOG2E - best)
    loss = best * LN2 + jnp.log(total) - target
    mine = loss[:, 0:share]
    for q in range(1, per):
        mine = jnp.where(lax.rem(me, per) == q, loss[:, q * share:(q + 1) * share], mine)
    out_ref[...] = mine


def body(embeddings, classifier, labels, row_scale):
    ndp, ncls = lax.axis_size("dp"), lax.axis_size("cls")
    assert ndp == 4 and ncls % 2 == 0
    ndev = ndp * ncls
    block, width = embeddings.shape
    rows = classifier.shape[0]
    count = labels.shape[0]
    piece = block // 4
    chunk = rows // 8
    groups = count // piece
    f32 = jnp.float32
    any_spec = pl.BlockSpec(memory_space=pl.ANY)
    vmem = pl.BlockSpec(memory_space=pltpu.VMEM)
    dma = pltpu.SemaphoreType.DMA
    out = pl.pallas_call(
        functools.partial(kernel, ndp, ncls, chunk),
        out_shape=jax.ShapeDtypeStruct((1, count // ndev), f32),
        in_specs=[any_spec, any_spec, pl.BlockSpec(memory_space=pltpu.SMEM), vmem, vmem],
        out_specs=vmem,
        scratch_shapes=[
            pltpu.VMEM((4, 2, block, width // 2), f32),
            pltpu.VMEM((rows, width), f32),
            pltpu.VMEM((rows, width), jnp.bfloat16),
            pltpu.VMEM((2 * piece, width), f32),
            pltpu.VMEM((2 * piece, width), jnp.bfloat16),
            pltpu.VMEM((chunk, 2 * piece), f32),
            pltpu.VMEM((chunk, 2 * piece), f32),
            pltpu.VMEM((groups, 8, piece), f32),
            pltpu.VMEM((ndev, 8, piece), f32),
            dma((2,)), dma((8,)), dma((6,)), dma((6,)), dma((6,)), dma((6,)),
            dma((12,)), dma((12,)), dma, dma,
        ],
        compiler_params=pltpu.CompilerParams(
            collective_id=0, has_side_effects=True, vmem_limit_bytes=56 * 1024 * 1024
        ),
    )(embeddings, classifier, labels, labels.reshape(groups, piece), row_scale.reshape(groups, piece))
    return out.reshape(count // ndev)


def solution(mesh):
    placed = (P("dp", None), P(("dp", "cls"), None), P(), P())
    return jax.shard_map(
        body, mesh=mesh, in_specs=placed, out_specs=P(("dp", "cls")), check_vma=False
    )
```

time: 239 us -> 50.8 us (0.21)
  blocking collectives: 80.4 us -> 0 us
  matrix products: 59.6 us -> 0 us
  Pallas kernels: 0 us -> 49.4 us
  other arithmetic: 35.8 us -> 0 us
  waiting for transfers between devices: 32.3 us -> 0 us
  local copies, waits for them, and re-layouts: 16.6 us -> 1.19 us
  between operations: 13.5 us -> 0.01 us
    dot_general x1 -> x0, matrix products: 59.6 us -> none  [block_stats(): lax.dot_general(units, rows, (((1,), (1,)), ((), ())), precision=lax.Prec...]
    pallas_call x0 -> x1, Pallas kernels: none -> 49.4 us  [body(): pl.pallas_call(functools.partial(kernel, ndp, ncls, chunk), out_shape=jax...]
    unnamed x1 -> x0, blocking collectives: 41.1 us -> none
    pmax x1 -> x0, blocking collectives: 39.3 us -> none  [body(): best = lax.pmax(peak, ('dp', 'cls'))]
    all_gather x1 -> x0, waiting for transfers between devices: 32.3 us -> none  [body(): lax.all_gather(units_mine, 'dp', axis=0, tiled=True)]
    reduce_sum x5 -> x0, other arithmetic: 28.3 us -> none  [the longest x1 15 us: block_stats(): total = jnp.sum(jnp.exp(logits - peak[:, None]), axis=1)]
    gather x1 -> x0, local copies, waits for them, and re-layouts: 13.7 us -> none  [body(): picked = jnp.take(normed, local_all, axis=0)]
    mul x3 -> x0, other arithmetic: 6.06 us -> none  [the longest x2 6.05 us: unit_rows(): values * lax.rsqrt(jnp.sum(values * values, axis=-1, keepdims=True) + 1e-06)]
  transfers between devices with their start and end apart: 1 -> 0, of which waited for: 1 -> 0; matrix products, arithmetic and copies ran while one was open for 9% -> 0% of each run, Pallas kernels for 0% -> 0%
where the time goes in v1:
time: 50.8 us; the launch traced here: 50.6 us
  Pallas kernels  49.4 us (97%)
  local copies, waits for them, and re-layouts  1.19 us (2%)
    pallas_call x1, Pallas kernels, body(): pl.pallas_call(functools.partial(kernel, ndp, ncls, chunk), out_shape=jax...  49.4 us
    unnamed x1, local copies, waits for them, and re-layouts  1.19 us

profile of v1, /device:TPU:0, one launch (start us, length us, event | category | flops | bytes accessed | tf_op | source)
XLA Modules:
  0.0 50.6 jit_solution(14703032781939617761)
XLA Ops:
  0.0 49.4 %shard_map.46 = f32[1,64]{1,0:T(1,128)} custom-call(f32[512,512]{1,0:T(8,128)} %emb_hbm.1, f32[4096,512]{1,0:T(8,128)} %cls_hbm.1, s32[2048]{0:T(1024)} %lab_sm.1, s32[16,128]{1,0:T(8,128)} %bitcast.3, f32[16,128]{1,0:T(8,128)} %bitcast.4), custom_call_target="tpu_custom_call" | custom-call | tf_op jit(solution)/shard_map/pallas_call | solution.py:233
  49.4 1.2 %copy.6 = f32[64]{0:T(128)} copy(f32[64]{0:T(128)} %bitcast.5) | data formatting | bytes 512
